TPU v7x, 256 devices: a 8x8x2 block of a 8x8x16 slice. The times are simulated.
256 devices in a mesh: grp: 2 (over z), row: 128 (over y, x, core).
Axes of the slice: x: 8, y: 8, z: 2, core: 2. Of those that a mesh axis runs over, the one named last changes fastest.
The devices are a block of a 8x8x16 slice.
Arguments:
- concentration: float32 [16, 1024, 1024], P('grp', 'row'), parts along dimension 0, may hold values from -0.95 to 1.35
- target_mass: float32 [16], P('grp'), parts along dimension 0, may hold values from 0 to 0.4
- mobility: float32 [16], P('grp'), parts along dimension 0, may hold values from 0.5 to 2
Outputs:
- updated: float32 [16, 1024, 1024], P('grp', 'row'), parts along dimension 0
- residual: float32 [16], P('grp'), parts along dimension 0
There are 2 independent parts, one for each index of `grp`. A program takes and returns all parts, laid end to end along the dimension named above; each array names one. Nothing has to cross between parts.
All inputs are finite; a program needn't handle non-finite values.
Results may differ from a plain program's by a relative error of at most 0.00005.
Values sent between devices are 32-bit elements; how exact they have to be, the bound alone decides.
A program may use at most 64 MiB of HBM per device.

v0:
```python
import math
import jax
import jax.numpy as jnp
from jax import lax
from jax.sharding import Mesh
from jax.sharding import PartitionSpec as P

ROW = ("row_0", "row_1", "row_2")
stiffness = 1.0
time_step = 0.05
stabilizer = 2.0


def by_axis(x, axes):
    for axis in axes:
        x = lax.psum(x, axis)
    return x


def make_tables(length):
    blocks = length // 128
    short_range = jnp.arange(blocks, dtype=jnp.int32)
    long_range = jnp.arange(128, dtype=jnp.int32)
    short_angle = (short_range[:, None] * short_range[None, :] % blocks).astype(jnp.float32) * (
        2.0 * math.pi / blocks
    )
    long_angle = (long_range[:, None] * long_range[None, :] % 128).astype(jnp.float32) * (
        2.0 * math.pi / 128
    )
    twist_angle = (short_range[:, None] * long_range[None, :]).astype(jnp.float32) * (
        2.0 * math.pi / length
    )
    return (
        jnp.cos(short_angle),
        jnp.sin(short_angle),
        jnp.cos(long_angle),
        jnp.sin(long_angle),
        jnp.cos(twist_angle),
        jnp.sin(twist_angle),
    )


def product(pattern, real_part, imag_part, cosine, sine, orient, real_only=False):

    def contract(operand, table):
        return jnp.einsum(pattern, operand, table, precision=lax.Precision.HIGHEST)

    if imag_part is None:
        return (contract(real_part, cosine), orient * contract(real_part, sine))
    if real_only:
        return (contract(real_part, cosine) - orient * contract(imag_part, sine), None)
    return (
        contract(real_part, cosine) - orient * contract(imag_part, sine),
        contract(imag_part, cosine) + orient * contract(real_part, sine),
    )


def rotate(real_part, imag_part, tables, orient):
    cosine, sine = (tables[4], tables[5])
    return (
        real_part * cosine - orient * imag_part * sine,
        imag_part * cosine + orient * real_part * sine,
    )


def forward_rows(real_field, tables, imag_field=None):
    planes, narrow, length = real_field.shape
    block_shape = (planes, narrow, length // 128, 128)
    shaped = real_field.reshape(block_shape)
    imag_shaped = None
    real_part, imag_part = product("pxab,ac->pxcb", shaped, imag_shaped, tables[0], tables[1], -1.0)
    real_part, imag_part = rotate(real_part, imag_part, tables, -1.0)
    real_part, imag_part = product(
        "pxcb,bd->pcdx", real_part, imag_part, tables[2], tables[3], -1.0
    )
    return (real_part.reshape(planes, length, narrow), imag_part.reshape(planes, length, narrow))


def forward_cols(pieces, tables):
    real_part, imag_part = pieces
    planes, narrow, length = real_part.shape
    shape = (planes, narrow, length // 128, 128)
    real_part, imag_part = product(
        "pqab,ac->pqcb",
        real_part.reshape(shape),
        imag_part.reshape(shape),
        tables[0],
        tables[1],
        -1.0,
    )
    real_part, imag_part = rotate(real_part, imag_part, tables, -1.0)
    real_part, imag_part = product(
        "pqcb,bd->pqcd", real_part, imag_part, tables[2], tables[3], -1.0
    )
    return (real_part.reshape(planes, narrow, length), imag_part.reshape(planes, narrow, length))


def inverse_cols(real_part, imag_part, tables):
    planes, narrow, length = real_part.shape
    shape = (planes, narrow, length // 128, 128)
    real_part, imag_part = product(
        "pqcd,db->pqcb",
        real_part.reshape(shape),
        imag_part.reshape(shape),
        tables[2],
        tables[3],
        1.0,
    )
    real_part, imag_part = rotate(real_part, imag_part, tables, 1.0)
    real_part, imag_part = product("pqcb,ca->pabq", real_part, imag_part, tables[0], tables[1], 1.0)
    return (real_part.reshape(planes, length, narrow), imag_part.reshape(planes, length, narrow))


def inverse_rows(pieces, tables):
    real_part, imag_part = pieces
    planes, narrow, length = real_part.shape
    shape = (planes, narrow, length // 128, 128)
    real_part, imag_part = product(
        "pxcd,db->pxcb",
        real_part.reshape(shape),
        imag_part.reshape(shape),
        tables[2],
        tables[3],
        1.0,
    )
    real_part, imag_part = rotate(real_part, imag_part, tables, 1.0)
    real_part, imag_part = product(
        "pxcb,ca->pxab", real_part, imag_part, tables[0], tables[1], 1.0, True
    )
    real_part = real_part.reshape(planes, narrow, length)
    return real_part


def digit_natural(positions, length):
    blocks = length // 128
    return positions // 128 + blocks * (positions % 128)


def wavenumbers(natural_index, length):
    signed = jnp.where(natural_index < length // 2, natural_index, natural_index - length)
    angular = signed.astype(jnp.float32) * (2.0 * math.pi / length)
    return (angular, jnp.where(natural_index == length // 2, jnp.float32(0.0), angular))


def local(concentration, target_mass, mobility):
    planes, rows_local, width_y = concentration.shape
    devices = lax.axis_size(ROW)
    width_x = rows_local * devices
    cols_local = width_y // devices
    cells = float(width_x * width_y)
    inverse_cells = 1.0 / cells
    residual = by_axis(jnp.sum(concentration, axis=(1, 2)), ROW) / cells - target_mass
    tables_y = make_tables(width_y)
    device = lax.axis_index(ROW)
    local_slots = jnp.arange(cols_local, dtype=jnp.int32)
    columns = device * cols_local + local_slots
    all_x = jnp.arange(width_x, dtype=jnp.int32)
    natural_x = digit_natural(all_x, width_x)
    angular_x, slope_x = wavenumbers(natural_x, width_x)
    angular_x, slope_x = (angular_x[None, :], slope_x[None, :])
    cubic_term = concentration * concentration * concentration - concentration

    def to_spectrum(pieces):
        return forward_cols(pieces, tables_y)

    angular_y, slope_y = wavenumbers(digit_natural(columns, width_y), width_y)
    stacked = jnp.concatenate([concentration, cubic_term], axis=0)
    half_real, half_imag = forward_rows(stacked, tables_y)
    spec_real, spec_imag = to_spectrum(
        (
            lax.all_to_all(half_real, ROW, split_axis=1, concat_axis=2, tiled=True),
            lax.all_to_all(half_imag, ROW, split_axis=1, concat_axis=2, tiled=True),
        )
    )
    field_real, field_imag = (spec_real[:planes], spec_imag[:planes])
    cubic_real, cubic_imag = (spec_real[planes:], spec_imag[planes:])
    angular_y, slope_y = (angular_y[:, None], slope_y[:, None])
    square = angular_x * angular_x + angular_y * angular_y
    chem_real = (cubic_real + stiffness * square * field_real) * inverse_cells
    chem_imag = (cubic_imag + stiffness * square * field_imag) * inverse_cells
    stack_real = jnp.concatenate([-slope_x * chem_imag, -slope_y * chem_imag], axis=0)
    stack_imag = jnp.concatenate([slope_x * chem_real, slope_y * chem_real], axis=0)
    back_real, back_imag = inverse_cols(stack_real, stack_imag, tables_y)
    gradient_pair = inverse_rows(
        (
            lax.all_to_all(back_real, ROW, split_axis=1, concat_axis=2, tiled=True),
            lax.all_to_all(back_imag, ROW, split_axis=1, concat_axis=2, tiled=True),
        ),
        tables_y,
    )
    grad_x = gradient_pair[:planes]
    grad_y = gradient_pair[planes:]
    weight = mobility[:, None, None] / (1.0 + concentration * concentration)
    fluxes = jnp.concatenate([weight * grad_x, weight * grad_y], axis=0)
    flux_half_real, flux_half_imag = forward_rows(fluxes, tables_y)
    flux_real, flux_imag = to_spectrum(
        (
            lax.all_to_all(flux_half_real, ROW, split_axis=1, concat_axis=2, tiled=True),
            lax.all_to_all(flux_half_imag, ROW, split_axis=1, concat_axis=2, tiled=True),
        )
    )
    flux_x_real, flux_x_imag = (flux_real[:planes], flux_imag[:planes])
    flux_y_real, flux_y_imag = (flux_real[planes:], flux_imag[planes:])
    div_real = -slope_x * flux_x_imag - slope_y * flux_y_imag
    div_imag = slope_x * flux_x_real + slope_y * flux_y_real
    factor = (
        time_step
        * inverse_cells
        / (
            1.0
            + time_step
            * mobility[:, None, None]
            * (stabilizer * square + stiffness * square * square)
        )
    )
    change_real, change_imag = inverse_cols(div_real * factor, div_imag * factor, tables_y)
    change = inverse_rows(
        (
            lax.all_to_all(change_real, ROW, split_axis=1, concat_axis=2, tiled=True),
            lax.all_to_all(change_imag, ROW, split_axis=1, concat_axis=2, tiled=True),
        ),
        tables_y,
    )
    fresh = concentration + change
    return (fresh - residual[:, None, None], residual)


def solution(mesh):
    torus = Mesh(
        mesh.devices.reshape(mesh.shape["grp"], 8, 8, 2), ("grp", "row_0", "row_1", "row_2")
    )
    in_specs = (P("grp", ROW, None), P("grp"), P("grp"))
    out_specs = (P("grp", ROW, None), P("grp"))
    return jax.shard_map(local, mesh=torus, in_specs=in_specs, out_specs=out_specs, check_vma=False)
```

profile of v0, /device:TPU:513, one launch (start us, length us, event | category | flops | bytes accessed | tf_op | source)
XLA Modules:
  0.0 410.4 jit_solution(5268577525299020385)
XLA Ops:
  9.3 4.2 %reshape.381 = f32[128,1,1024]{2,1,0:T(1,128)} reshape(f32[1024,8,16]{2,1,0:T(8,128)} %bitcast.296) | data formatting | bytes 1048576
  13.5 28.1 %all-to-all-start.1 = ((f32[128,1,1024]{2,1,0:T(1,128)}), f32[128,1,1024]{2,1,0:T(1,128)S(1)}, u32[]{:S(2)}, u32[]{:S(2)}) async-start(f32[128,1,1024]{2,1,0:T(1,128)} %reshape.381), calls=%async_computation.1 | async-start | bytes 1048576 | tf_op jit(solution)/shard_map/all_to_all | solution.py:171
  50.8 10.3 %all-to-all-done.1 = f32[128,1,1024]{2,1,0:T(1,128)S(1)} async-done(((f32[128,1,1024]{2,1,0:T(1,128)}), f32[128,1,1024]{2,1,0:T(1,128)S(1)}, u32[]{:S(2)}, u32[]{:S(2)}) %all-to-all-start.1) | async-done | bytes 524320 | tf_op jit(solution)/shard_map/all_to_all | solution.py:171
  61.0 7.5 %all-to-all-start = ((f32[128,1,1024]{2,1,0:T(1,128)}), f32[128,1,1024]{2,1,0:T(1,128)S(1)}, u32[]{:S(2)}, u32[]{:S(2)}) async-start(f32[128,1,1024]{2,1,0:T(1,128)} %reshape.383), calls=%async_computation | async-start | bytes 1048576 | tf_op jit(solution)/shard_map/all_to_all | solution.py:172
  73.9 4.4 %copy.115 = f32[16,8,128,8]{0,3,2,1:T(8,128)} copy(f32[16,8,128,8]{0,3,1,2:T(8,128)} %bitcast.302) | data formatting | bytes 1048576 | tf_op jit(solution)/shard_map/all_to_all | solution.py:171
  81.8 6.3 %all-to-all-done = f32[128,1,1024]{2,1,0:T(1,128)S(1)} async-done(((f32[128,1,1024]{2,1,0:T(1,128)}), f32[128,1,1024]{2,1,0:T(1,128)S(1)}, u32[]{:S(2)}, u32[]{:S(2)}) %all-to-all-start) | async-done | bytes 524320 | tf_op jit(solution)/shard_map/all_to_all | solution.py:172
  92.7 4.4 %copy.109 = f32[16,8,128,8]{0,3,2,1:T(8,128)} copy(f32[16,8,128,8]{0,3,1,2:T(8,128)} %bitcast.304) | data formatting | bytes 1048576 | tf_op jit(solution)/shard_map/all_to_all | solution.py:172
  117.7 10.1 %all-to-all-start.2 = ((f32[128,1,1024]{2,1,0:T(1,128)}), f32[128,1,1024]{2,1,0:T(1,128)S(1)}, u32[]{:S(2)}, u32[]{:S(2)}) async-start(f32[128,1,1024]{2,1,0:T(1,128)} %reshape.387), calls=%async_computation.2 | async-start | bytes 1048576 | tf_op jit(solution)/shard_map/all_to_all | solution.py:186
  132.1 4.2 %reshape.385 = f32[128,1,1024]{2,1,0:T(1,128)} reshape(f32[1024,8,16]{2,1,0:T(8,128)} %bitcast.299) | data formatting | bytes 1048576
  136.3 11.1 %all-to-all-done.2 = f32[128,1,1024]{2,1,0:T(1,128)S(1)} async-done(((f32[128,1,1024]{2,1,0:T(1,128)}), f32[128,1,1024]{2,1,0:T(1,128)S(1)}, u32[]{:S(2)}, u32[]{:S(2)}) %all-to-all-start.2) | async-done | bytes 524320 | tf_op jit(solution)/shard_map/all_to_all | solution.py:186
  147.4 7.5 %all-to-all-start.3 = ((f32[128,1,1024]{2,1,0:T(1,128)}), f32[128,1,1024]{2,1,0:T(1,128)S(1)}, u32[]{:S(2)}, u32[]{:S(2)}) async-start(f32[128,1,1024]{2,1,0:T(1,128)} %reshape.385), calls=%async_computation.3 | async-start | bytes 1048576 | tf_op jit(solution)/shard_map/all_to_all | solution.py:187
  162.2 6.7 %fusion.104 = f32[16,8,8,128]{3,0,2,1:T(8,128)S(1)} fusion(f32[16,8,8,128]{0,3,2,1:T(8,128)S(1)} %bitcast.292), kind=kOutput, calls=%fused_computation.167 | convolution fusion | flops 201555968 | bytes 1048576 | tf_op jit(solution)/shard_map/pxcd,db->pxcb/dot_general | solution.py:46
  168.9 6.7 %fusion.128 = f32[16,8,8,128]{3,0,2,1:T(8,128)S(1)} fusion(f32[16,8,8,128]{0,3,2,1:T(8,128)S(1)} %bitcast.293), kind=kOutput, calls=%fused_computation.191 | convolution fusion | flops 201555968 | bytes 1048576 | tf_op jit(solution)/shard_map/pxcd,db->pxcb/dot_general | solution.py:46
  183.1 6.7 %fusion.106 = f32[16,8,8,128]{3,0,2,1:T(8,128)S(1)} fusion(f32[16,8,8,128]{0,3,2,1:T(8,128)S(1)} %bitcast.294), kind=kOutput, calls=%fused_computation.169 | convolution fusion | flops 201555968 | bytes 1048576 | tf_op jit(solution)/shard_map/pxcd,db->pxcb/dot_general | solution.py:46
  189.8 6.7 %fusion.126 = f32[16,8,8,128]{3,0,2,1:T(8,128)S(1)} fusion(f32[16,8,8,128]{0,3,2,1:T(8,128)S(1)} %bitcast.295), kind=kOutput, calls=%fused_computation.189 | convolution fusion | flops 201555968 | bytes 1048576 | tf_op jit(solution)/shard_map/pxcd,db->pxcb/dot_general | solution.py:46
  206.5 4.2 %reshape.389 = f32[128,1,1024]{2,1,0:T(1,128)} reshape(f32[1024,8,16]{2,1,0:T(8,128)} %bitcast.300) | data formatting | bytes 1048576
  210.7 17.1 %all-to-all-start.5 = ((f32[128,1,1024]{2,1,0:T(1,128)}), f32[128,1,1024]{2,1,0:T(1,128)S(1)}, u32[]{:S(2)}, u32[]{:S(2)}) async-start(f32[128,1,1024]{2,1,0:T(1,128)} %reshape.389), calls=%async_computation.5 | async-start | bytes 1048576 | tf_op jit(solution)/shard_map/all_to_all | solution.py:198
  237.0 9.9 %all-to-all-done.5 = f32[128,1,1024]{2,1,0:T(1,128)S(1)} async-done(((f32[128,1,1024]{2,1,0:T(1,128)}), f32[128,1,1024]{2,1,0:T(1,128)S(1)}, u32[]{:S(2)}, u32[]{:S(2)}) %all-to-all-start.5) | async-done | bytes 524320 | tf_op jit(solution)/shard_map/all_to_all | solution.py:198
  247.0 7.5 %all-to-all-start.4 = ((f32[128,1,1024]{2,1,0:T(1,128)}), f32[128,1,1024]{2,1,0:T(1,128)S(1)}, u32[]{:S(2)}, u32[]{:S(2)}) async-start(f32[128,1,1024]{2,1,0:T(1,128)} %reshape.391), calls=%async_computation.4 | async-start | bytes 1048576 | tf_op jit(solution)/shard_map/all_to_all | solution.py:199
  259.1 4.4 %copy.141 = f32[16,8,128,8]{0,3,2,1:T(8,128)} copy(f32[16,8,128,8]{0,3,1,2:T(8,128)} %bitcast.308) | data formatting | bytes 1048576 | tf_op jit(solution)/shard_map/all_to_all | solution.py:198
  267.0 7.0 %all-to-all-done.4 = f32[128,1,1024]{2,1,0:T(1,128)S(1)} async-done(((f32[128,1,1024]{2,1,0:T(1,128)}), f32[128,1,1024]{2,1,0:T(1,128)S(1)}, u32[]{:S(2)}, u32[]{:S(2)}) %all-to-all-start.4) | async-done | bytes 524320 | tf_op jit(solution)/shard_map/all_to_all | solution.py:199
  278.7 4.4 %copy.135 = f32[16,8,128,8]{0,3,2,1:T(8,128)} copy(f32[16,8,128,8]{0,3,1,2:T(8,128)} %bitcast.310) | data formatting | bytes 1048576 | tf_op jit(solution)/shard_map/all_to_all | solution.py:199
  297.9 4.5 %reshape.395 = f32[128,1,512]{2,1,0:T(1,128)} reshape(f32[1024,8,8]{2,1,0:T(8,128)} %bitcast.312) | data formatting | bytes 524288
  302.4 9.3 %all-to-all-start.6 = ((f32[128,1,512]{2,1,0:T(1,128)}), f32[128,1,512]{2,1,0:T(1,128)S(1)}, u32[]{:S(2)}, u32[]{:S(2)}) async-start(f32[128,1,512]{2,1,0:T(1,128)} %reshape.395), calls=%async_computation.6 | async-start | bytes 524288 | tf_op jit(solution)/shard_map/all_to_all | solution.py:219
  315.6 4.5 %reshape.393 = f32[128,1,512]{2,1,0:T(1,128)} reshape(f32[1024,8,8]{2,1,0:T(8,128)} %bitcast.313) | data formatting | bytes 524288
  320.1 5.9 %all-to-all-done.6 = f32[128,1,512]{2,1,0:T(1,128)S(1)} async-done(((f32[128,1,512]{2,1,0:T(1,128)}), f32[128,1,512]{2,1,0:T(1,128)S(1)}, u32[]{:S(2)}, u32[]{:S(2)}) %all-to-all-start.6) | async-done | bytes 262176 | tf_op jit(solution)/shard_map/all_to_all | solution.py:219
  326.0 10.4 %all-to-all-start.7 = ((f32[128,1,512]{2,1,0:T(1,128)}), f32[128,1,512]{2,1,0:T(1,128)S(1)}, u32[]{:S(2)}, u32[]{:S(2)}) async-start(f32[128,1,512]{2,1,0:T(1,128)} %reshape.393), calls=%async_computation.7 | async-start | bytes 524288 | tf_op jit(solution)/shard_map/all_to_all | solution.py:220
  336.4 16.2 %psum.21 = f32[8]{0:T(128)S(1)} all-reduce(f32[8]{0:T(128)S(1)} %get-tuple-element.14), channel_id=1, replica_groups=mesh['grp'=2,'row_0'=8,'row_1'=8,'row_2'=2] {'row_0'}, use_global_device_ids=true, to_apply=%region_1.0 | all-reduce | flops 8 | bytes 64 | tf_op jit(solution)/shard_map/psum | solution.py:16
  352.6 12.9 %psum.22 = f32[8]{0:T(128)S(1)} all-reduce(f32[8]{0:T(128)S(1)} %psum.21), channel_id=1, replica_groups=mesh['grp'=2,'row_0'=8,'row_1'=8,'row_2'=2] {'row_1'}, use_global_device_ids=true, to_apply=%region_2.0 | all-reduce | flops 8 | bytes 64 | tf_op jit(solution)/shard_map/psum | solution.py:16
  365.5 9.7 %psum.23 = f32[8]{0:T(128)S(1)} all-reduce(f32[8]{0:T(128)S(1)} %psum.22), channel_id=1, replica_groups=mesh['grp'=2,'row_0'=8,'row_1'=8,'row_2'=2] {'row_2'}, use_global_device_ids=true, to_apply=%region_3.0 | all-reduce | flops 8 | bytes 64 | tf_op jit(solution)/shard_map/psum | solution.py:16
  380.1 6.6 %copy.147 = f32[8,8,128,8]{3,2,1,0:T(8,128)} copy(f32[8,8,128,8]{3,0,1,2:T(8,128)} %bitcast.314) | data formatting | bytes 524288 | tf_op jit(solution)/shard_map/all_to_all | solution.py:219
  395.8 6.6 %copy.150 = f32[8,8,128,8]{3,2,1,0:T(8,128)} copy(f32[8,8,128,8]{3,0,1,2:T(8,128)} %bitcast.315) | data formatting | bytes 524288 | tf_op jit(solution)/shard_map/all_to_all | solution.py:220
  (123 shorter events, 142.6 us)
Async XLA Ops:
  13.5 47.6 %all-to-all-start.1 = ((f32[128,1,1024]{2,1,0:T(1,128)}), f32[128,1,1024]{2,1,0:T(1,128)S(1)}, u32[]{:S(2)}, u32[]{:S(2)}) async-start(f32[128,1,1024]{2,1,0:T(1,128)} %reshape.381), calls=%async_computation.1 | async-start | bytes 1048576 | tf_op jit(solution)/shard_map/all_to_all | solution.py:171
  61.0 27.1 %all-to-all-start = ((f32[128,1,1024]{2,1,0:T(1,128)}), f32[128,1,1024]{2,1,0:T(1,128)S(1)}, u32[]{:S(2)}, u32[]{:S(2)}) async-start(f32[128,1,1024]{2,1,0:T(1,128)} %reshape.383), calls=%async_computation | async-start | bytes 1048576 | tf_op jit(solution)/shard_map/all_to_all | solution.py:172
  117.7 29.7 %all-to-all-start.2 = ((f32[128,1,1024]{2,1,0:T(1,128)}), f32[128,1,1024]{2,1,0:T(1,128)S(1)}, u32[]{:S(2)}, u32[]{:S(2)}) async-start(f32[128,1,1024]{2,1,0:T(1,128)} %reshape.387), calls=%async_computation.2 | async-start | bytes 1048576 | tf_op jit(solution)/shard_map/all_to_all | solution.py:186
  147.4 28.2 %all-to-all-start.3 = ((f32[128,1,1024]{2,1,0:T(1,128)}), f32[128,1,1024]{2,1,0:T(1,128)S(1)}, u32[]{:S(2)}, u32[]{:S(2)}) async-start(f32[128,1,1024]{2,1,0:T(1,128)} %reshape.385), calls=%async_computation.3 | async-start | bytes 1048576 | tf_op jit(solution)/shard_map/all_to_all | solution.py:187
  196.5 3.4 copy-start
  196.5 3.4 copy-start.1
  210.7 36.3 %all-to-all-start.5 = ((f32[128,1,1024]{2,1,0:T(1,128)}), f32[128,1,1024]{2,1,0:T(1,128)S(1)}, u32[]{:S(2)}, u32[]{:S(2)}) async-start(f32[128,1,1024]{2,1,0:T(1,128)} %reshape.389), calls=%async_computation.5 | async-start | bytes 1048576 | tf_op jit(solution)/shard_map/all_to_all | solution.py:198
  247.0 27.1 %all-to-all-start.4 = ((f32[128,1,1024]{2,1,0:T(1,128)}), f32[128,1,1024]{2,1,0:T(1,128)S(1)}, u32[]{:S(2)}, u32[]{:S(2)}) async-start(f32[128,1,1024]{2,1,0:T(1,128)} %reshape.391), calls=%async_computation.4 | async-start | bytes 1048576 | tf_op jit(solution)/shard_map/all_to_all | solution.py:199
  302.4 23.6 %all-to-all-start.6 = ((f32[128,1,512]{2,1,0:T(1,128)}), f32[128,1,512]{2,1,0:T(1,128)S(1)}, u32[]{:S(2)}, u32[]{:S(2)}) async-start(f32[128,1,512]{2,1,0:T(1,128)} %reshape.395), calls=%async_computation.6 | async-start | bytes 524288 | tf_op jit(solution)/shard_map/all_to_all | solution.py:219
  312.5 62.7 %copy-start.3 = (f32[8]{0:T(128)S(1)}, f32[8]{0:T(128)}, u32[]{:S(2)}) copy-start(f32[8]{0:T(128)} %param.4) | copy-start | bytes 100
  326.0 64.9 %all-to-all-start.7 = ((f32[128,1,512]{2,1,0:T(1,128)}), f32[128,1,512]{2,1,0:T(1,128)S(1)}, u32[]{:S(2)}, u32[]{:S(2)}) async-start(f32[128,1,512]{2,1,0:T(1,128)} %reshape.393), calls=%async_computation.7 | async-start | bytes 524288 | tf_op jit(solution)/shard_map/all_to_all | solution.py:220
  375.2 33.9 %copy-start.2 = (f32[8]{0:T(128)}, f32[8]{0:T(128)S(1)}, u32[]{:S(2)}) copy-start(f32[8]{0:T(128)S(1)} %multiply_subtract_fusion.13) | copy-start | bytes 100
where the time goes:
time: 418 us; the launch traced here: 410 us
  local copies, waits for them, and re-layouts  139 us (33%)
  starting transfers between devices  97.4 us (23%)
  matrix products  65.4 us (16%)
  waiting for transfers between devices  50.5 us (12%)
  blocking collectives  38.8 us (9%)
  other arithmetic  17.4 us (4%)
    dot_general x56, matrix products, contract(): return jnp.einsum(pattern, operand, table, precision=lax.Precision.HIGHEST)  65.4 us
    unnamed x24, local copies, waits for them, and re-layouts  58.3 us
    psum x3, blocking collectives, by_axis(): x = lax.psum(x, axis)  38.8 us
    all_to_all x1, starting transfers between devices, local(): lax.all_to_all(half_real, ROW, split_axis=1, concat_axis=2, tiled=True)  28.1 us
    all_to_all x1, starting transfers between devices, local(): lax.all_to_all(flux_half_real, ROW, split_axis=1, concat_axis=2, tiled=True)  17.1 us
    all_to_all x1, waiting for transfers between devices, local(): lax.all_to_all(back_real, ROW, split_axis=1, concat_axis=2, tiled=True)  11.1 us
    all_to_all x1, starting transfers between devices, local(): lax.all_to_all(change_imag, ROW, split_axis=1, concat_axis=2, tiled=True)  10.4 us
    all_to_all x1, waiting for transfers between devices, local(): lax.all_to_all(half_real, ROW, split_axis=1, concat_axis=2, tiled=True)  10.3 us
  transfers between devices with their start and end apart: 8, of which 6 were waited for; matrix products, arithmetic and copies ran while one was open for 24% of the time, Pallas kernels for 0%

commit v1 on v0

--- a/solution.py
+++ b/solution.py
@@ -1,3 +1,4 @@
+import functools
 import math
 import jax
 import jax.numpy as jnp
@@ -9,6 +10,17 @@
 stiffness = 1.0
 time_step = 0.05
 stabilizer = 2.0
+
+
+def step_on_spots_over_axis(z_in, axis_no, ndim_at):
+    f_next = lax.axis_size(ROW)
+    mid_arr = lax.all_to_all(
+        jnp.stack(jnp.split(z_in, f_next, axis=axis_no)), ROW, concat_axis=0, split_axis=0
+    )
+    return jnp.concatenate(mid_arr, axis=ndim_at)
+
+
+_take_bench = functools.partial(step_on_spots_over_axis, axis_no=1, ndim_at=2)
 
 
 def by_axis(x, axes):
@@ -168,7 +180,7 @@
     half_real, half_imag = forward_rows(stacked, tables_y)
     spec_real, spec_imag = to_spectrum(
         (
-            lax.all_to_all(half_real, ROW, split_axis=1, concat_axis=2, tiled=True),
+            _take_bench(half_real),
             lax.all_to_all(half_imag, ROW, split_axis=1, concat_axis=2, tiled=True),
         )
     )

time: 418 us -> 521 us (1.25)
  local copies, waits for them, and re-layouts: 139 us -> 241 us
    unnamed x24 -> x151, local copies, waits for them, and re-layouts: 58.3 us -> 147 us
    another operation x0 -> x3, local copies, waits for them, and re-layouts: none -> 10.4 us  [the longest x2 7.54 us: step_on_spots_over_axis(): jnp.stack(jnp.split(z_in, f_next, axis=axis_no))]
    reshape x2, local copies, waits for them, and re-layouts: 6.34 us -> 14.6 us  [forward_cols(): imag_part.reshape(shape)]
  transfers between devices with their start and end apart: 8 -> 8, of which waited for: 6 -> 6; matrix products, arithmetic and copies ran while one was open for 24% -> 19% of each run, Pallas kernels for 0% -> 0%
where the time goes in v1:
time: 521 us; the launch traced here: 513 us
  local copies, waits for them, and re-layouts  241 us (46%)
  starting transfers between devices  97.4 us (19%)
  matrix products  65.4 us (13%)
  waiting for transfers between devices  50.6 us (10%)
  blocking collectives  38.8 us (7%)
  other arithmetic  17.4 us (3%)
    unnamed x151, local copies, waits for them, and re-layouts  147 us
    dot_general x56, matrix products, contract(): return jnp.einsum(pattern, operand, table, precision=lax.Precision.HIGHEST)  65.4 us
    psum x3, blocking collectives, by_axis(): x = lax.psum(x, axis)  38.8 us
    all_to_all x1, starting transfers between devices, step_on_spots_over_axis(): lax.all_to_all(jnp.stack(jnp.split(z_in, f_next, axis=axis_no)), ROW, con...  27.7 us
    all_to_all x1, starting transfers between devices, local(): lax.all_to_all(flux_half_real, ROW, split_axis=1, concat_axis=2, tiled=True)  17.1 us
    reshape x2, local copies, waits for them, and re-layouts, forward_cols(): imag_part.reshape(shape)  14.6 us
    all_to_all x1, waiting for transfers between devices, local(): lax.all_to_all(back_real, ROW, split_axis=1, concat_axis=2, tiled=True)  11.1 us
    all_to_all x1, waiting for transfers between devices, step_on_spots_over_axis(): lax.all_to_all(jnp.stack(jnp.split(z_in, f_next, axis=axis_no)), ROW, con...  10.6 us
  transfers between devices with their start and end apart: 8, of which 6 were waited for; matrix products, arithmetic and copies ran while one was open for 19% of the time, Pallas kernels for 0%

profile of v1, /device:TPU:513, one launch (start us, length us, event | category | flops | bytes accessed | tf_op | source)
XLA Modules:
  0.0 512.5 jit_solution(2314567108999219435)
XLA Ops:
  95.9 6.8 %copy.541 = f32[128,16,8,8]{1,3,2,0:T(8,128)} copy(f32[128,16,8,8]{2,3,1,0:T(8,128)} %constant_dynamic-update-slice_fusion) | data formatting | bytes 1048576 | tf_op jit(solution)/shard_map/stack | solution.py:18
  106.9 27.7 %all-to-all-start.1 = ((f32[128,1,1024]{2,1,0:T(1,128)}), f32[128,1,1024]{2,1,0:T(1,128)S(1)}, u32[]{:S(2)}, u32[]{:S(2)}) async-start(f32[128,1,1024]{2,1,0:T(1,128)} %reshape.380), calls=%async_computation.1 | async-start | bytes 1048576 | tf_op jit(solution)/shard_map/all_to_all | solution.py:17
  139.7 4.2 reshape.382
  143.9 10.6 %all-to-all-done.1 = f32[128,1,1024]{2,1,0:T(1,128)S(1)} async-done(((f32[128,1,1024]{2,1,0:T(1,128)}), f32[128,1,1024]{2,1,0:T(1,128)S(1)}, u32[]{:S(2)}, u32[]{:S(2)}) %all-to-all-start.1) | async-done | bytes 524320 | tf_op jit(solution)/shard_map/all_to_all | solution.py:17
  154.5 7.5 %all-to-all-start = ((f32[128,1,1024]{2,1,0:T(1,128)}), f32[128,1,1024]{2,1,0:T(1,128)S(1)}, u32[]{:S(2)}, u32[]{:S(2)}) async-start(f32[128,1,1024]{2,1,0:T(1,128)} %reshape.382), calls=%async_computation | async-start | bytes 1048576 | tf_op jit(solution)/shard_map/all_to_all | solution.py:184
  175.5 6.1 %all-to-all-done = f32[128,1,1024]{2,1,0:T(1,128)S(1)} async-done(((f32[128,1,1024]{2,1,0:T(1,128)}), f32[128,1,1024]{2,1,0:T(1,128)S(1)}, u32[]{:S(2)}, u32[]{:S(2)}) %all-to-all-start) | async-done | bytes 524320 | tf_op jit(solution)/shard_map/all_to_all | solution.py:184
  186.3 4.4 copy.536
  190.7 11.6 %copy.537 = f32[16,8,8,128]{3,2,1,0:T(8,128)S(1)} copy(f32[16,8,8,128]{0,3,2,1:T(8,128)} %bitcast.944) | data formatting | bytes 1048576 | tf_op jit(solution)/shard_map/reshape | solution.py:98
  219.5 10.4 %all-to-all-start.2 = ((f32[128,1,1024]{2,1,0:T(1,128)}), f32[128,1,1024]{2,1,0:T(1,128)S(1)}, u32[]{:S(2)}, u32[]{:S(2)}) async-start(f32[128,1,1024]{2,1,0:T(1,128)} %reshape.386), calls=%async_computation.2 | async-start | bytes 1048576 | tf_op jit(solution)/shard_map/all_to_all | solution.py:198
  234.2 4.2 reshape.384
  238.4 11.1 %all-to-all-done.2 = f32[128,1,1024]{2,1,0:T(1,128)S(1)} async-done(((f32[128,1,1024]{2,1,0:T(1,128)}), f32[128,1,1024]{2,1,0:T(1,128)S(1)}, u32[]{:S(2)}, u32[]{:S(2)}) %all-to-all-start.2) | async-done | bytes 524320 | tf_op jit(solution)/shard_map/all_to_all | solution.py:198
  249.4 7.5 %all-to-all-start.3 = ((f32[128,1,1024]{2,1,0:T(1,128)}), f32[128,1,1024]{2,1,0:T(1,128)S(1)}, u32[]{:S(2)}, u32[]{:S(2)}) async-start(f32[128,1,1024]{2,1,0:T(1,128)} %reshape.384), calls=%async_computation.3 | async-start | bytes 1048576 | tf_op jit(solution)/shard_map/all_to_all | solution.py:199
  264.5 6.7 %fusion.104 = f32[16,8,8,128]{3,0,2,1:T(8,128)S(1)} fusion(f32[16,8,8,128]{0,3,2,1:T(8,128)S(1)} %bitcast.932), kind=kOutput, calls=%fused_computation.423 | convolution fusion | flops 201555968 | bytes 1048576 | tf_op jit(solution)/shard_map/pxcd,db->pxcb/dot_general | solution.py:58
  271.1 6.7 %fusion.128 = f32[16,8,8,128]{3,0,2,1:T(8,128)S(1)} fusion(f32[16,8,8,128]{0,3,2,1:T(8,128)S(1)} %bitcast.933), kind=kOutput, calls=%fused_computation.447 | convolution fusion | flops 201555968 | bytes 1048576 | tf_op jit(solution)/shard_map/pxcd,db->pxcb/dot_general | solution.py:58
  285.1 6.7 %fusion.106 = f32[16,8,8,128]{3,0,2,1:T(8,128)S(1)} fusion(f32[16,8,8,128]{0,3,2,1:T(8,128)S(1)} %bitcast.934), kind=kOutput, calls=%fused_computation.425 | convolution fusion | flops 201555968 | bytes 1048576 | tf_op jit(solution)/shard_map/pxcd,db->pxcb/dot_general | solution.py:58
  291.9 6.7 %fusion.126 = f32[16,8,8,128]{3,0,2,1:T(8,128)S(1)} fusion(f32[16,8,8,128]{0,3,2,1:T(8,128)S(1)} %bitcast.935), kind=kOutput, calls=%fused_computation.445 | convolution fusion | flops 201555968 | bytes 1048576 | tf_op jit(solution)/shard_map/pxcd,db->pxcb/dot_general | solution.py:58
  312.8 17.1 %all-to-all-start.5 = ((f32[128,1,1024]{2,1,0:T(1,128)}), f32[128,1,1024]{2,1,0:T(1,128)S(1)}, u32[]{:S(2)}, u32[]{:S(2)}) async-start(f32[128,1,1024]{2,1,0:T(1,128)} %reshape.388), calls=%async_computation.5 | async-start | bytes 1048576 | tf_op jit(solution)/shard_map/all_to_all | solution.py:210
  339.2 9.9 %all-to-all-done.5 = f32[128,1,1024]{2,1,0:T(1,128)S(1)} async-done(((f32[128,1,1024]{2,1,0:T(1,128)}), f32[128,1,1024]{2,1,0:T(1,128)S(1)}, u32[]{:S(2)}, u32[]{:S(2)}) %all-to-all-start.5) | async-done | bytes 524320 | tf_op jit(solution)/shard_map/all_to_all | solution.py:210
  349.1 7.5 %all-to-all-start.4 = ((f32[128,1,1024]{2,1,0:T(1,128)}), f32[128,1,1024]{2,1,0:T(1,128)S(1)}, u32[]{:S(2)}, u32[]{:S(2)}) async-start(f32[128,1,1024]{2,1,0:T(1,128)} %reshape.390), calls=%async_computation.4 | async-start | bytes 1048576 | tf_op jit(solution)/shard_map/all_to_all | solution.py:211
  361.3 4.4 copy.568
  369.2 7.0 %all-to-all-done.4 = f32[128,1,1024]{2,1,0:T(1,128)S(1)} async-done(((f32[128,1,1024]{2,1,0:T(1,128)}), f32[128,1,1024]{2,1,0:T(1,128)S(1)}, u32[]{:S(2)}, u32[]{:S(2)}) %all-to-all-start.4) | async-done | bytes 524320 | tf_op jit(solution)/shard_map/all_to_all | solution.py:211
  380.8 4.4 copy.562
  400.1 4.5 reshape.394
  404.6 9.3 %all-to-all-start.6 = ((f32[128,1,512]{2,1,0:T(1,128)}), f32[128,1,512]{2,1,0:T(1,128)S(1)}, u32[]{:S(2)}, u32[]{:S(2)}) async-start(f32[128,1,512]{2,1,0:T(1,128)} %reshape.394), calls=%async_computation.6 | async-start | bytes 524288 | tf_op jit(solution)/shard_map/all_to_all | solution.py:231
  417.8 4.5 reshape.392
  422.2 5.9 %all-to-all-done.6 = f32[128,1,512]{2,1,0:T(1,128)S(1)} async-done(((f32[128,1,512]{2,1,0:T(1,128)}), f32[128,1,512]{2,1,0:T(1,128)S(1)}, u32[]{:S(2)}, u32[]{:S(2)}) %all-to-all-start.6) | async-done | bytes 262176 | tf_op jit(solution)/shard_map/all_to_all | solution.py:231
  428.2 10.4 %all-to-all-start.7 = ((f32[128,1,512]{2,1,0:T(1,128)}), f32[128,1,512]{2,1,0:T(1,128)S(1)}, u32[]{:S(2)}, u32[]{:S(2)}) async-start(f32[128,1,512]{2,1,0:T(1,128)} %reshape.392), calls=%async_computation.7 | async-start | bytes 524288 | tf_op jit(solution)/shard_map/all_to_all | solution.py:232
  438.5 16.2 %psum.21 = f32[8]{0:T(128)S(1)} all-reduce(f32[8]{0:T(128)S(1)} %get-tuple-element.14), channel_id=1, replica_groups=mesh['grp'=2,'row_0'=8,'row_1'=8,'row_2'=2] {'row_0'}, use_global_device_ids=true, to_apply=%region_1.0 | all-reduce | flops 8 | bytes 64 | tf_op jit(solution)/shard_map/psum | solution.py:28
  454.7 12.9 %psum.22 = f32[8]{0:T(128)S(1)} all-reduce(f32[8]{0:T(128)S(1)} %psum.21), channel_id=1, replica_groups=mesh['grp'=2,'row_0'=8,'row_1'=8,'row_2'=2] {'row_1'}, use_global_device_ids=true, to_apply=%region_2.0 | all-reduce | flops 8 | bytes 64 | tf_op jit(solution)/shard_map/psum | solution.py:28
  467.6 9.7 %psum.23 = f32[8]{0:T(128)S(1)} all-reduce(f32[8]{0:T(128)S(1)} %psum.22), channel_id=1, replica_groups=mesh['grp'=2,'row_0'=8,'row_1'=8,'row_2'=2] {'row_2'}, use_global_device_ids=true, to_apply=%region_3.0 | all-reduce | flops 8 | bytes 64 | tf_op jit(solution)/shard_map/psum | solution.py:28
  482.2 6.6 %copy.574 = f32[8,8,128,8]{3,2,1,0:T(8,128)} copy(f32[8,8,128,8]{3,0,1,2:T(8,128)} %bitcast.953) | data formatting | bytes 524288 | tf_op jit(solution)/shard_map/all_to_all | solution.py:231
  497.9 6.6 %copy.577 = f32[8,8,128,8]{3,2,1,0:T(8,128)} copy(f32[8,8,128,8]{3,0,1,2:T(8,128)} %bitcast.954) | data formatting | bytes 524288 | tf_op jit(solution)/shard_map/all_to_all | solution.py:232
  (252 shorter events, 234.8 us)
Async XLA Ops:
  106.9 47.6 %all-to-all-start.1 = ((f32[128,1,1024]{2,1,0:T(1,128)}), f32[128,1,1024]{2,1,0:T(1,128)S(1)}, u32[]{:S(2)}, u32[]{:S(2)}) async-start(f32[128,1,1024]{2,1,0:T(1,128)} %reshape.380), calls=%async_computation.1 | async-start | bytes 1048576 | tf_op jit(solution)/shard_map/all_to_all | solution.py:17
  154.5 27.1 %all-to-all-start = ((f32[128,1,1024]{2,1,0:T(1,128)}), f32[128,1,1024]{2,1,0:T(1,128)S(1)}, u32[]{:S(2)}, u32[]{:S(2)}) async-start(f32[128,1,1024]{2,1,0:T(1,128)} %reshape.382), calls=%async_computation | async-start | bytes 1048576 | tf_op jit(solution)/shard_map/all_to_all | solution.py:184
  219.5 30.0 %all-to-all-start.2 = ((f32[128,1,1024]{2,1,0:T(1,128)}), f32[128,1,1024]{2,1,0:T(1,128)S(1)}, u32[]{:S(2)}, u32[]{:S(2)}) async-start(f32[128,1,1024]{2,1,0:T(1,128)} %reshape.386), calls=%async_computation.2 | async-start | bytes 1048576 | tf_op jit(solution)/shard_map/all_to_all | solution.py:198
  249.4 28.4 %all-to-all-start.3 = ((f32[128,1,1024]{2,1,0:T(1,128)}), f32[128,1,1024]{2,1,0:T(1,128)S(1)}, u32[]{:S(2)}, u32[]{:S(2)}) async-start(f32[128,1,1024]{2,1,0:T(1,128)} %reshape.384), calls=%async_computation.3 | async-start | bytes 1048576 | tf_op jit(solution)/shard_map/all_to_all | solution.py:199
  285.1 16.8 %copy-start = (f32[8,8,1024]{2,1,0:T(8,128)S(1)}, f32[8,8,1024]{2,1,0:T(8,128)}, u32[]{:S(2)}) copy-start(f32[8,8,1024]{2,1,0:T(8,128)} %param.3) | copy-start | bytes 786436
  285.1 16.8 %copy-start.1 = (f32[8]{0:T(128)S(1)}, f32[8]{0:T(128)}, u32[]{:S(2)}) copy-start(f32[8]{0:T(128)} %param.5) | copy-start | bytes 100
  312.8 36.3 %all-to-all-start.5 = ((f32[128,1,1024]{2,1,0:T(1,128)}), f32[128,1,1024]{2,1,0:T(1,128)S(1)}, u32[]{:S(2)}, u32[]{:S(2)}) async-start(f32[128,1,1024]{2,1,0:T(1,128)} %reshape.388), calls=%async_computation.5 | async-start | bytes 1048576 | tf_op jit(solution)/shard_map/all_to_all | solution.py:210
  349.1 27.1 %all-to-all-start.4 = ((f32[128,1,1024]{2,1,0:T(1,128)}), f32[128,1,1024]{2,1,0:T(1,128)S(1)}, u32[]{:S(2)}, u32[]{:S(2)}) async-start(f32[128,1,1024]{2,1,0:T(1,128)} %reshape.390), calls=%async_computation.4 | async-start | bytes 1048576 | tf_op jit(solution)/shard_map/all_to_all | solution.py:211
  400.1 77.3 %copy-start.3 = (f32[8]{0:T(128)S(1)}, f32[8]{0:T(128)}, u32[]{:S(2)}) copy-start(f32[8]{0:T(128)} %param.4) | copy-start | bytes 100
  404.6 23.6 %all-to-all-start.6 = ((f32[128,1,512]{2,1,0:T(1,128)}), f32[128,1,512]{2,1,0:T(1,128)S(1)}, u32[]{:S(2)}, u32[]{:S(2)}) async-start(f32[128,1,512]{2,1,0:T(1,128)} %reshape.394), calls=%async_computation.6 | async-start | bytes 524288 | tf_op jit(solution)/shard_map/all_to_all | solution.py:231
  428.2 64.9 %all-to-all-start.7 = ((f32[128,1,512]{2,1,0:T(1,128)}), f32[128,1,512]{2,1,0:T(1,128)S(1)}, u32[]{:S(2)}, u32[]{:S(2)}) async-start(f32[128,1,512]{2,1,0:T(1,128)} %reshape.392), calls=%async_computation.7 | async-start | bytes 524288 | tf_op jit(solution)/shard_map/all_to_all | solution.py:232
  477.3 33.9 %copy-start.2 = (f32[8]{0:T(128)}, f32[8]{0:T(128)S(1)}, u32[]{:S(2)}) copy-start(f32[8]{0:T(128)S(1)} %multiply_subtract_fusion.13) | copy-start | bytes 100
